TPU v7x, 32 devices: a whole 2x2x4 slice. The times are simulated.
32 devices in a mesh: tm: 16 (over z, y, core), chan: 2 (over x).
Axes of the slice: x: 2, y: 2, z: 4, core: 2. Of those that a mesh axis runs over, the one named last changes fastest.
Arguments:
- signal: bfloat16 [32768, 512], P('tm', 'chan'), may hold values from -72 to 72
- tapers: bfloat16 [8, 4096], replicated, may hold values from -0.09375 to 0.09375
- eigenvalues: float32 [8], replicated, may hold values from 0.05 to 1
Outputs:
- relative_psd: float32 [2048, 512], P('tm', 'chan')
All inputs are finite; a program needn't handle non-finite values.
Results may differ from a plain program's by a relative error of at most 0.0026.
The roundings to bfloat16 on the way count: a program that leaves them out, or rounds other values in their place, can miss the bound.
Values may be sent and summed in bfloat16 or wider, within the bound.
No kernel may reach another device: no remote copies, remote signals or barrier semaphores. Data moves between devices by JAX's collectives and lax.ppermute only.
A program may use at most 64 MiB of HBM per device.

v0:
```python
import math
import jax
import jax.numpy as jnp
from jax import lax
from jax.sharding import PartitionSpec as P

P_SIZE = 32
Q = 128
EPSILON = 1e-06


def dft_tables(outer_size, inner_size):
    inner = jnp.arange(inner_size, dtype=jnp.int32)
    outer = jnp.arange(outer_size, dtype=jnp.int32)
    halves = jnp.arange(outer_size // 2, dtype=jnp.int32)
    angle_first = (inner[:, None] * inner[None, :] % inner_size).astype(jnp.float32) * (
        2.0 * math.pi / inner_size
    )
    first_table = jnp.concatenate([jnp.cos(angle_first), -jnp.sin(angle_first)], axis=0).astype(
        jnp.bfloat16
    )
    angle_twist = (inner[:, None] * outer[None, :] % (outer_size * inner_size)).astype(
        jnp.float32
    ) * (2.0 * math.pi / (outer_size * inner_size))
    twist_cos = jnp.cos(angle_twist)[:, :, None, None]
    twist_sin = jnp.sin(angle_twist)[:, :, None, None]
    angle_last = (outer[:, None] * halves[None, :] % outer_size).astype(jnp.float32) * (
        2.0 * math.pi / outer_size
    )
    last_cos = jnp.cos(angle_last).astype(jnp.bfloat16)
    last_sin = jnp.sin(angle_last).astype(jnp.bfloat16)
    return (first_table, twist_cos, twist_sin, last_cos, last_sin)


def taper_power(tapered, tables):
    first_table, twist_cos, twist_sin, last_cos, last_sin = tables
    inner_size = tapered.shape[0]
    first = jnp.einsum("jn,npsc->jpsc", first_table, tapered, preferred_element_type=jnp.float32)
    first_real = first[:inner_size]
    first_imaginary = first[inner_size:]
    twist_real = (first_real * twist_cos + first_imaginary * twist_sin).astype(jnp.bfloat16)
    twist_imaginary = (first_imaginary * twist_cos - first_real * twist_sin).astype(jnp.bfloat16)
    last_real = jnp.einsum(
        "pa,kpsc->aksc", last_cos, twist_real, preferred_element_type=jnp.float32
    ) + jnp.einsum("pa,kpsc->aksc", last_sin, twist_imaginary, preferred_element_type=jnp.float32)
    last_imaginary = jnp.einsum(
        "pa,kpsc->aksc", last_cos, twist_imaginary, preferred_element_type=jnp.float32
    ) - jnp.einsum("pa,kpsc->aksc", last_sin, twist_real, preferred_element_type=jnp.float32)
    return last_real * last_real + last_imaginary * last_imaginary


def local(signal, tapers, eigenvalues):
    row_count, chan_count = signal.shape
    outer_size = P_SIZE
    inner_size = Q
    stride = tapers.shape[1] // 2
    half_inner = inner_size // 2
    tm_size = lax.axis_size("tm")
    samples = signal.astype(jnp.float32)
    common = lax.psum(jnp.sum(samples, axis=1), "chan") / (chan_count * lax.axis_size("chan"))
    referenced = (samples - common[:, None]).astype(jnp.bfloat16)
    all_rows = row_count * tm_size
    segments = all_rows // stride - 1
    tables = dft_tables(outer_size, inner_size)
    weights = eigenvalues / jnp.sum(eigenvalues)
    taper_grid = tapers.reshape(tapers.shape[0], inner_size, outer_size, 1, 1)
    columns = lax.all_to_all(referenced, "tm", split_axis=1, concat_axis=0, tiled=True)
    narrow = columns.shape[1]
    widened = columns.astype(jnp.float32)
    centre = jnp.sum(widened, axis=0) / all_rows
    variance = jnp.sum((widened - centre) ** 2, axis=0) / all_rows
    halves = columns.reshape(all_rows // stride, half_inner, outer_size, narrow)
    halves = jnp.transpose(halves, (1, 2, 0, 3))
    windows = jnp.concatenate([halves[:, :, :-1], halves[:, :, 1:]], axis=0)

    def add_column_taper(taper, accumulated):
        taper_row = lax.dynamic_index_in_dim(taper_grid, taper, 0, keepdims=False).astype(
            jnp.float32
        )
        tapered = ((windows.astype(jnp.float32) - centre) * taper_row).astype(jnp.bfloat16)
        power = taper_power(tapered, tables)
        return accumulated + weights[taper] * jnp.sum(power, axis=2).reshape(stride, narrow)

    total = lax.fori_loop(
        0, tapers.shape[0], add_column_taper, jnp.zeros((stride, narrow), jnp.float32)
    )
    density = total / segments / (variance + EPSILON)
    return lax.all_to_all(density, "tm", split_axis=0, concat_axis=1, tiled=True)


def solution(mesh):
    return jax.shard_map(
        local,
        mesh=mesh,
        in_specs=(P("tm", "chan"), P(), P()),
        out_specs=P("tm", "chan"),
        check_vma=False,
    )
```

profile of v0, /device:TPU:0, one launch (start us, length us, event | category | flops | bytes accessed | tf_op | source)
XLA Modules:
  0.0 131.2 jit_solution(6070422819959520975)
XLA Ops:
  0.0 1.5 %copy.30 = bf16[2048,256]{0,1:T(8,128)(2,1)S(1)} copy(bf16[2048,256]{1,0:T(8,128)(2,1)} %param.5) | data formatting | bytes 2097152 | tf_op args[0]
  1.7 5.9 %psum.7 = f32[2048]{0:T(1024)S(1)} all-reduce(f32[2048]{0:T(1024)S(1)} %convert_reduce_fusion.1), channel_id=1, replica_groups=mesh['tm'=16,'chan'=2] {'chan'}, use_global_device_ids=true, to_apply=%region_1.0 | all-reduce | flops 2048 | bytes 16384 | tf_op jit(solution)/shard_map/psum | solution.py:60
  7.6 1.2 fusion.55
  8.8 6.5 %all-to-all-start = ((bf16[2048,16,16]{0,2,1:T(8,128)(2,1)}), bf16[2048,16,16]{0,2,1:T(8,128)(2,1)S(1)}, u32[]{:S(2)}, u32[]{:S(2)}) async-start(bf16[2048,16,16]{0,2,1:T(8,128)(2,1)} %bitcast), calls=%async_computation | async-start | bytes 2097152 | tf_op jit(solution)/shard_map/all_to_all | solution.py:67
  15.7 0.7 reduce_sum.49
  16.7 0.7 broadcast_divide_fusion
  17.4 20.9 %all-to-all-done = bf16[2048,16,16]{0,2,1:T(8,128)(2,1)S(1)} async-done(((bf16[2048,16,16]{0,2,1:T(8,128)(2,1)}), bf16[2048,16,16]{0,2,1:T(8,128)(2,1)S(1)}, u32[]{:S(2)}, u32[]{:S(2)}) %all-to-all-start) | async-done | bytes 1048608 | tf_op jit(solution)/shard_map/all_to_all | solution.py:67
  38.6 0.6 fusion.57
  39.2 4.4 %reshape.113 = bf16[16,64,32,16]{2,1,3,0:T(8,128)(2,1)} reshape(bf16[16,2048,16]{1,2,0:T(8,128)(2,1)S(1)} %bitcast.71) | data formatting | bytes 2097152 | tf_op jit(solution)/shard_map/reshape | solution.py:72
  43.6 7.0 %fusion.64 = (bf16[64,32,15,16]{1,0,3,2:T(8,128)(2,1)}, bf16[64,32,15,16]{1,0,3,2:T(8,128)(2,1)}) fusion(bf16[64,32,16,16]{1,0,3,2:T(8,128)(2,1)} %bitcast.70), kind=kLoop, calls=%fused_computation.89 | loop fusion | bytes 3932160 | tf_op jit(solution)/shard_map/slice | solution.py:74
  50.6 5.8 %copy.31 = bf16[64,32,15,16]{0,3,2,1:T(8,128)(2,1)} copy(bf16[64,32,15,16]{1,0,3,2:T(8,128)(2,1)} %get-tuple-element.308) | data formatting | bytes 1966080 | tf_op jit(solution)/shard_map/slice | solution.py:74
  56.5 5.8 %copy.32 = bf16[64,32,15,16]{0,3,2,1:T(8,128)(2,1)} copy(bf16[64,32,15,16]{1,0,3,2:T(8,128)(2,1)} %get-tuple-element.309) | data formatting | bytes 1966080 | tf_op jit(solution)/shard_map/slice | solution.py:74
  62.2 3.2 %pad_maximum_fusion = bf16[128,32,15,16]{0,3,2,1:T(8,128)(2,1)S(1)} fusion(bf16[64,32,15,16]{0,3,2,1:T(8,128)(2,1)} %copy.32, bf16[64,32,15,16]{0,3,2,1:T(8,128)(2,1)} %copy.31), kind=kLoop, calls=%fused_computation.70 | loop fusion | flops 3932160 | bytes 3932160 | tf_op jit(solution)/shard_map/concatenate | solution.py:74
  65.4 50.4 %while.15 = (s32[]{:T(128)}, f32[2048,16]{0,1:T(8,128)S(1)}, f32[8]{0:T(128)S(1)}, bf16[128,32,15,16]{0,3,2,1:T(8,128)(2,1)S(1)}, f32[16]{0:T(128)S(1)}, /*index...) while((s32[]{:T(128)}, f32[2048,16]{0,1:T(8,128)S(1)}, ...), condition=%wide.region_6.7_spmd.clone.clone, body=%wide.region_4.6_spmd.clone.clone.sunk | while | flops 644048896 | bytes 42246336 | solution.py:84
  65.5 0.7 dynamic_slice.23
  66.2 1.2 convolution_bitcast_fusion.2
  67.4 1.1 add_convert_fusion.2
  70.0 0.9 add_reduce_fusion.2
  70.9 0.7 broadcast_multiply_fusion.4
  71.7 0.7 dynamic_slice.23
  72.5 1.2 convolution_bitcast_fusion.2
  73.7 1.1 add_convert_fusion.2
  75.3 0.5 fusion.86
  75.8 0.5 fusion.87
  76.3 0.9 add_reduce_fusion.2
  77.2 0.7 broadcast_multiply_fusion.4
  78.0 0.7 dynamic_slice.23
  78.8 1.2 convolution_bitcast_fusion.2
  80.0 1.1 add_convert_fusion.2
  82.6 0.9 add_reduce_fusion.2
  83.5 0.7 broadcast_multiply_fusion.4
  84.3 0.7 dynamic_slice.23
  85.1 1.2 convolution_bitcast_fusion.2
  86.3 1.1 add_convert_fusion.2
  87.9 0.5 fusion.86
  88.4 0.5 fusion.87
  88.9 0.9 add_reduce_fusion.2
  89.8 0.7 broadcast_multiply_fusion.4
  90.6 0.7 dynamic_slice.23
  91.4 1.2 convolution_bitcast_fusion.2
  92.6 1.1 add_convert_fusion.2
  95.2 0.9 add_reduce_fusion.2
  96.1 0.7 broadcast_multiply_fusion.4
  96.9 0.7 dynamic_slice.23
  97.7 1.2 convolution_bitcast_fusion.2
  98.9 1.1 add_convert_fusion.2
  100.5 0.5 fusion.86
  101.0 0.5 fusion.87
  101.5 0.9 add_reduce_fusion.2
  102.4 0.7 broadcast_multiply_fusion.4
  103.2 0.7 dynamic_slice.23
  104.0 1.2 convolution_bitcast_fusion.2
  105.2 1.1 add_convert_fusion.2
  107.8 0.9 add_reduce_fusion.2
  108.7 0.7 broadcast_multiply_fusion.4
  109.5 0.7 dynamic_slice.23
  110.3 1.2 convolution_bitcast_fusion.2
  111.5 1.1 add_convert_fusion.2
  113.1 0.5 fusion.86
  113.6 0.5 fusion.87
  114.1 0.9 add_reduce_fusion.2
  115.0 0.7 broadcast_multiply_fusion.4
  115.9 14.5 %all_to_all.35 = f32[16,128,16]{1,2,0:T(8,128)S(1)} all-to-all(f32[16,128,16]{1,2,0:T(8,128)S(1)} %copy_bitcast_fusion), channel_id=1, replica_groups=mesh['tm'=16,'chan'=2] {'tm'}, dimensions={0} | all-to-all | bytes 262144 | tf_op jit(solution)/shard_map/all_to_all | solution.py:88
  130.4 0.8 copy.35
  (55 shorter events, 10.4 us)
Async XLA Ops:
  7.6 7.7 %copy-start = (bf16[8,4096]{1,0:T(8,128)(2,1)S(1)}, bf16[8,4096]{1,0:T(8,128)(2,1)}, u32[]{:S(2)}) copy-start(bf16[8,4096]{1,0:T(8,128)(2,1)} %param.6) | copy-start | bytes 196612
  7.6 8.1 %copy-start.1 = (f32[8]{0:T(128)S(1)}, f32[8]{0:T(128)}, u32[]{:S(2)}) copy-start(f32[8]{0:T(128)} %param.7) | copy-start | bytes 100
  8.8 29.4 %all-to-all-start = ((bf16[2048,16,16]{0,2,1:T(8,128)(2,1)}), bf16[2048,16,16]{0,2,1:T(8,128)(2,1)S(1)}, u32[]{:S(2)}, u32[]{:S(2)}) async-start(bf16[2048,16,16]{0,2,1:T(8,128)(2,1)} %bitcast), calls=%async_computation | async-start | bytes 2097152 | tf_op jit(solution)/shard_map/all_to_all | solution.py:67
where the time goes:
time: 132 us; the launch traced here: 131 us
  local copies, waits for them, and re-layouts  30.9 us (23%)
  matrix products  28.8 us (22%)
  other arithmetic  23.2 us (18%)
  waiting for transfers between devices  20.9 us (16%)
  blocking collectives  20.4 us (15%)
  starting transfers between devices  6.47 us (5%)
    all_to_all x1, waiting for transfers between devices, local(): lax.all_to_all(referenced, 'tm', split_axis=1, concat_axis=0, tiled=True)  20.9 us
    slice x3, local copies, waits for them, and re-layouts, local(): windows = jnp.concatenate([halves[:, :, :-1], halves[:, :, 1:]], axis=0)  18.6 us
    all_to_all x1, blocking collectives, local(): lax.all_to_all(density, 'tm', split_axis=0, concat_axis=1, tiled=True)  14.5 us
    dot_general x8, matrix products, taper_power(): jnp.einsum('jn,npsc->jpsc', first_table, tapered, preferred_element_type=...  9.85 us
    convert_element_type x8, other arithmetic, taper_power(): (first_real * twist_cos + first_imaginary * twist_sin).astype(jnp.bfloat16)  8.88 us
    dot_general x8, matrix products, taper_power(): jnp.einsum('pa,kpsc->aksc', last_sin, twist_real, preferred_element_type=...  7.2 us
    all_to_all x1, starting transfers between devices, local(): lax.all_to_all(referenced, 'tm', split_axis=1, concat_axis=0, tiled=True)  6.47 us
    psum x1, blocking collectives, local(): lax.psum(jnp.sum(samples, axis=1), 'chan')  5.94 us
  transfers between devices with their start and end apart: 1, of which 1 were waited for; matrix products, arithmetic and copies ran while one was open for 2% of the time, Pallas kernels for 0%

commit v1 on v0

--- a/solution.py
+++ b/solution.py
@@ -64,7 +64,10 @@
     tables = dft_tables(outer_size, inner_size)
     weights = eigenvalues / jnp.sum(eigenvalues)
     taper_grid = tapers.reshape(tapers.shape[0], inner_size, outer_size, 1, 1)
-    columns = lax.all_to_all(referenced, "tm", split_axis=1, concat_axis=0, tiled=True)
+    columns = jnp.concatenate(
+        lax.all_to_all(jnp.stack(jnp.split(referenced, lax.axis_size("tm"), axis=1)), "tm", 0, 0),
+        axis=0,
+    )
     narrow = columns.shape[1]
     widened = columns.astype(jnp.float32)
     centre = jnp.sum(widened, axis=0) / all_rows

time: 132 us -> 141 us (1.068)
  local copies, waits for them, and re-layouts: 30.9 us -> 40.9 us
    unnamed x6 -> x21, local copies, waits for them, and re-layouts: 1.62 us -> 11 us
    another operation x0 -> x2, local copies, waits for them, and re-layouts: none -> 5.09 us  [the longest x1 4.45 us: local(): halves = columns.reshape(all_rows // stride, half_inner, outer_size, narrow)]
    reshape x1 -> x0, local copies, waits for them, and re-layouts: 4.45 us -> none  [local(): halves = columns.reshape(all_rows // stride, half_inner, outer_size, narrow)]
  transfers between devices with their start and end apart: 1 -> 1, of which waited for: 1 -> 1; matrix products, arithmetic and copies ran while one was open for 2% -> 1% of each run, Pallas kernels for 0% -> 0%
where the time goes in v1:
time: 141 us
  local copies, waits for them, and re-layouts  40.9 us (29%)
  matrix products  28.7 us (20%)
  other arithmetic  22.9 us (16%)
  waiting for transfers between devices  20.9 us (15%)
  blocking collectives  20.4 us (14%)
  starting transfers between devices  6.47 us (5%)
    all_to_all x1, waiting for transfers between devices, local(): lax.all_to_all(jnp.stack(jnp.split(referenced, lax.axis_size('tm'), axis=...  20.9 us
    slice x3, local copies, waits for them, and re-layouts, local(): windows = jnp.concatenate([halves[:, :, :-1], halves[:, :, 1:]], axis=0)  18.6 us
    all_to_all x1, blocking collectives, local(): lax.all_to_all(density, 'tm', split_axis=0, concat_axis=1, tiled=True)  14.5 us
    unnamed x21, local copies, waits for them, and re-layouts  11 us
    dot_general x8, matrix products, taper_power(): jnp.einsum('jn,npsc->jpsc', first_table, tapered, preferred_element_type=...  9.84 us
    convert_element_type x8, other arithmetic, taper_power(): (first_real * twist_cos + first_imaginary * twist_sin).astype(jnp.bfloat16)  9.58 us
    dot_general x8, matrix products, taper_power(): jnp.einsum('pa,kpsc->aksc', last_sin, twist_real, preferred_element_type=...  7.2 us
    all_to_all x1, starting transfers between devices, local(): lax.all_to_all(jnp.stack(jnp.split(referenced, lax.axis_size('tm'), axis=...  6.47 us
  transfers between devices with their start and end apart: 1, of which 1 were waited for; matrix products, arithmetic and copies ran while one was open for 1% of the time, Pallas kernels for 0%

profile of v1, /device:TPU:0, one launch (start us, length us, event | category | flops | bytes accessed | tf_op | source)
XLA Modules:
  0.0 141.0 jit_solution(3581902538525283963)
XLA Ops:
  0.0 1.5 %copy.30 = bf16[2048,256]{0,1:T(8,128)(2,1)S(1)} copy(bf16[2048,256]{1,0:T(8,128)(2,1)} %param.5) | data formatting | bytes 2097152 | tf_op args[0]
  1.7 5.9 %psum.7 = f32[2048]{0:T(1024)S(1)} all-reduce(f32[2048]{0:T(1024)S(1)} %convert_reduce_fusion.1), channel_id=1, replica_groups=mesh['tm'=16,'chan'=2] {'chan'}, use_global_device_ids=true, to_apply=%region_1.0 | all-reduce | flops 2048 | bytes 16384 | tf_op jit(solution)/shard_map/psum | solution.py:60
  7.8 0.6 fusion.76
  9.1 0.6 fusion.74
  11.0 0.6 fusion.71
  11.6 0.6 fusion.70
  12.8 0.6 fusion.68
  13.5 0.6 fusion.67
  14.1 0.6 fusion.66
  16.0 0.6 fusion.63
  16.6 0.6 fusion.62
  17.2 0.6 fusion.61
  17.8 6.5 %all-to-all-start = ((bf16[16,2048,16]{1,2,0:T(8,128)(2,1)}), bf16[16,2048,16]{1,2,0:T(8,128)(2,1)S(1)}, u32[]{:S(2)}, u32[]{:S(2)}) async-start(bf16[16,2048,16]{1,2,0:T(8,128)(2,1)} %fusion.61), calls=%async_computation | async-start | bytes 2097152 | tf_op jit(solution)/shard_map/all_to_all | solution.py:68
  24.7 0.7 reduce_sum.49
  25.6 0.7 broadcast_divide_fusion
  26.4 20.9 %all-to-all-done = bf16[16,2048,16]{1,2,0:T(8,128)(2,1)S(1)} async-done(((bf16[16,2048,16]{1,2,0:T(8,128)(2,1)}), bf16[16,2048,16]{1,2,0:T(8,128)(2,1)S(1)}, u32[]{:S(2)}, u32[]{:S(2)}) %all-to-all-start) | async-done | bytes 1048608 | tf_op jit(solution)/shard_map/all_to_all | solution.py:68
  48.2 4.4 %reshape_reshape.3 = bf16[16,64,32,16]{2,1,3,0:T(8,128)(2,1)} reshape(bf16[16,2048,16]{1,2,0:T(8,128)(2,1)S(1)} %all-to-all-done) | data formatting | bytes 2097152 | tf_op jit(solution)/shard_map/reshape;reshape | solution.py:75
  52.6 7.0 %fusion.80 = (bf16[64,32,15,16]{1,0,3,2:T(8,128)(2,1)}, bf16[64,32,15,16]{1,0,3,2:T(8,128)(2,1)}) fusion(bf16[64,32,16,16]{1,0,3,2:T(8,128)(2,1)} %bitcast.130), kind=kLoop, calls=%fused_computation.121 | loop fusion | bytes 3932160 | tf_op jit(solution)/shard_map/slice | solution.py:77
  59.6 5.8 %copy.31 = bf16[64,32,15,16]{0,3,2,1:T(8,128)(2,1)} copy(bf16[64,32,15,16]{1,0,3,2:T(8,128)(2,1)} %get-tuple-element.308) | data formatting | bytes 1966080 | tf_op jit(solution)/shard_map/slice | solution.py:77
  65.4 5.8 %copy.32 = bf16[64,32,15,16]{0,3,2,1:T(8,128)(2,1)} copy(bf16[64,32,15,16]{1,0,3,2:T(8,128)(2,1)} %get-tuple-element.309) | data formatting | bytes 1966080 | tf_op jit(solution)/shard_map/slice | solution.py:77
  71.2 3.2 %pad_maximum_fusion = bf16[128,32,15,16]{0,3,2,1:T(8,128)(2,1)S(1)} fusion(bf16[64,32,15,16]{0,3,2,1:T(8,128)(2,1)} %copy.32, bf16[64,32,15,16]{0,3,2,1:T(8,128)(2,1)} %copy.31), kind=kLoop, calls=%fused_computation.70 | loop fusion | flops 3932160 | bytes 3932160 | tf_op jit(solution)/shard_map/concatenate | solution.py:77
  74.4 51.2 %while.15 = (s32[]{:T(128)}, f32[2048,16]{0,1:T(8,128)S(1)}, f32[8]{0:T(128)S(1)}, bf16[128,32,15,16]{0,3,2,1:T(8,128)(2,1)S(1)}, f32[16]{0:T(128)S(1)}, /*index...) while((s32[]{:T(128)}, f32[2048,16]{0,1:T(8,128)S(1)}, ...), condition=%wide.region_6.7_spmd.clone.clone, body=%wide.region_4.6_spmd.clone.clone.sunk | while | flops 644048896 | bytes 42246328 | solution.py:87
  74.5 1.2 convolution_bitcast_fusion.2
  75.8 1.2 add_convert_fusion.2
  78.5 0.9 add_reduce_fusion.2
  79.4 0.7 dynamic_slice.23
  80.0 0.7 broadcast_multiply_fusion.4
  80.9 1.2 convolution_bitcast_fusion.2
  82.2 1.2 add_convert_fusion.2
  84.9 0.9 add_reduce_fusion.2
  85.8 0.7 dynamic_slice.23
  86.5 0.7 broadcast_multiply_fusion.4
  87.3 1.2 convolution_bitcast_fusion.2
  88.6 1.2 add_convert_fusion.2
  91.3 0.9 add_reduce_fusion.2
  92.2 0.7 dynamic_slice.23
  92.9 0.7 broadcast_multiply_fusion.4
  93.7 1.2 convolution_bitcast_fusion.2
  95.0 1.2 add_convert_fusion.2
  97.7 0.9 add_reduce_fusion.2
  98.6 0.7 dynamic_slice.23
  99.2 0.7 broadcast_multiply_fusion.4
  100.1 1.2 convolution_bitcast_fusion.2
  101.4 1.2 add_convert_fusion.2
  104.1 0.9 add_reduce_fusion.2
  105.0 0.7 dynamic_slice.23
  105.6 0.7 broadcast_multiply_fusion.4
  106.5 1.2 convolution_bitcast_fusion.2
  107.8 1.2 add_convert_fusion.2
  110.4 0.9 add_reduce_fusion.2
  111.4 0.7 dynamic_slice.23
  112.0 0.7 broadcast_multiply_fusion.4
  112.9 1.2 convolution_bitcast_fusion.2
  114.2 1.2 add_convert_fusion.2
  116.8 0.9 add_reduce_fusion.2
  117.7 0.7 dynamic_slice.23
  118.4 0.7 broadcast_multiply_fusion.4
  119.2 1.2 convolution_bitcast_fusion.2
  120.6 1.2 add_convert_fusion.2
  123.2 0.9 add_reduce_fusion.2
  124.1 0.7 dynamic_slice.23
  124.8 0.7 broadcast_multiply_fusion.4
  125.7 14.5 %all_to_all.24 = f32[16,128,16]{1,2,0:T(8,128)S(1)} all-to-all(f32[16,128,16]{1,2,0:T(8,128)S(1)} %copy_bitcast_fusion), channel_id=1, replica_groups=mesh['tm'=16,'chan'=2] {'tm'}, dimensions={0} | all-to-all | bytes 262144 | tf_op jit(solution)/shard_map/all_to_all | solution.py:91
  140.2 0.8 copy.35
  (71 shorter events, 18.9 us)
Async XLA Ops:
  9.1 15.2 %copy-start = (bf16[8,4096]{1,0:T(8,128)(2,1)S(1)}, bf16[8,4096]{1,0:T(8,128)(2,1)}, u32[]{:S(2)}) copy-start(bf16[8,4096]{1,0:T(8,128)(2,1)} %param.6) | copy-start | bytes 196612
  12.2 12.4 %copy-start.1 = (f32[8]{0:T(128)S(1)}, f32[8]{0:T(128)}, u32[]{:S(2)}) copy-start(f32[8]{0:T(128)} %param.7) | copy-start | bytes 100
  17.8 29.4 %all-to-all-start = ((bf16[16,2048,16]{1,2,0:T(8,128)(2,1)}), bf16[16,2048,16]{1,2,0:T(8,128)(2,1)S(1)}, u32[]{:S(2)}, u32[]{:S(2)}) async-start(bf16[16,2048,16]{1,2,0:T(8,128)(2,1)} %fusion.61), calls=%async_computation | async-start | bytes 2097152 | tf_op jit(solution)/shard_map/all_to_all | solution.py:68
